TPU v7x, 32 devices: a whole 2x2x4 slice. The times are simulated.
32 devices in a mesh: dp: 8 (over y, x, core), mp: 4 (over z).
Axes of the slice: x: 2, y: 2, z: 4, core: 2. Of those that a mesh axis runs over, the one named last changes fastest.
Arguments:
- tokens: bfloat16 [4096, 1024], P('dp', 'mp'), may hold values from -150 to 150
- pre_gain: bfloat16 [1024], P('mp'), may hold values from 0.25 to 1.75
- input_weight: bfloat16 [3, 1024, 1024], P(None, 'dp', 'mp'), may hold values from -0.125 to 0.125
- output_weight: bfloat16 [1024, 1024], P('mp', 'dp'), may hold values from -1 to 1
- position_bias: bfloat16 [16, 512, 512], P('mp'), may hold values from -3 to 353
- post_gain: bfloat16 [1024], P('mp'), may hold values from 0.25 to 1.75
Outputs:
- stream: bfloat16 [4096, 1024], P('dp', 'mp')
- normed: bfloat16 [4096, 1024], P('dp', 'mp')
All inputs are finite; a program needn't handle non-finite values.
Results may differ from a plain program's by a relative error of at most 0.013.
Values may be sent and summed in bfloat16 or wider, within the bound.
A program may use at most 64 MiB of HBM per device.

v0:
```python
import jax
import jax.numpy as jnp
from jax import lax
from jax.sharding import PartitionSpec as P

epsilon = 1e-06


def attend_all(mixed_heads, position_bias):
    row_count = mixed_heads.shape[1]
    inner_width = mixed_heads.shape[2]
    head_count = position_bias.shape[0]
    seq_len = position_bias.shape[1]
    grouped = mixed_heads.reshape(
        3, row_count // seq_len, seq_len, head_count, inner_width // head_count
    )
    bias_wide = position_bias.astype(jnp.float32)

    def one_sequence(sequence):
        sequence_block = lax.dynamic_index_in_dim(grouped, sequence, 1, keepdims=False)
        scores = (
            jnp.einsum(
                "qhd,khd->hqk",
                sequence_block[0],
                sequence_block[1],
                preferred_element_type=jnp.float32,
            )
            + bias_wide
        )
        row_max = jnp.max(scores, axis=2, keepdims=True)
        weights = jnp.exp(scores - row_max)
        probabilities = (weights / jnp.sum(weights, axis=2, keepdims=True)).astype(jnp.bfloat16)
        context = jnp.einsum(
            "hqk,khd->qhd", probabilities, sequence_block[2], preferred_element_type=jnp.float32
        )
        return context.reshape(seq_len, inner_width).astype(jnp.bfloat16)

    stacked = lax.map(one_sequence, jnp.arange(row_count // seq_len, dtype=jnp.int32))
    return stacked.reshape(row_count, inner_width)


def on_device(tokens, pre_gain, input_weight, output_weight, position_bias, post_gain):
    rows_all, gain_all = (
        lax.all_gather(tokens, "mp", axis=1, tiled=True),
        lax.all_gather(pre_gain, "mp", axis=0, tiled=True),
    )
    widened = rows_all.astype(jnp.float32)
    inverse_rms = lax.rsqrt(jnp.mean(widened * widened, axis=1, keepdims=True) + epsilon)
    normed_in = (widened * inverse_rms * gain_all.astype(jnp.float32)).astype(jnp.bfloat16)
    feature_count = tokens.shape[1]
    projected = jnp.einsum(
        "td,kdi->kti",
        normed_in,
        lax.all_gather(input_weight, "dp", axis=1, tiled=True),
        preferred_element_type=jnp.float32,
    )
    context = attend_all(projected.astype(jnp.bfloat16), position_bias)
    partial_value = jnp.dot(
        context,
        lax.all_gather(output_weight, "dp", axis=1, tiled=True),
        preferred_element_type=jnp.float32,
    )
    attention_out = lax.psum_scatter(
        partial_value.astype(jnp.bfloat16), "mp", scatter_dimension=1, tiled=True
    ).astype(jnp.float32)
    stream = (tokens.astype(jnp.float32) + attention_out).astype(jnp.bfloat16)
    restored = lax.optimization_barrier(stream).astype(jnp.float32)
    squares = lax.psum(jnp.sum(restored * restored, axis=1), "mp")
    post_rms = lax.rsqrt(squares[:, None] / (feature_count * lax.axis_size("mp")) + epsilon)
    normed = (restored * post_rms * post_gain.astype(jnp.float32)).astype(jnp.bfloat16)
    return (stream, normed)


def solution(mesh):
    return jax.shard_map(
        on_device,
        mesh=mesh,
        in_specs=(
            P("dp", "mp"),
            P("mp"),
            P(None, "dp", "mp"),
            P("mp", "dp"),
            P("mp", None, None),
            P("mp"),
        ),
        out_specs=(P("dp", "mp"), P("dp", "mp")),
        check_vma=False,
    )
```

profile of v0, /device:TPU:0, one launch (start us, length us, event | category | flops | bytes accessed | tf_op | source)
XLA Modules:
  0.0 123.4 jit_solution(2190378064825369234)
XLA Ops:
  7.2 0.0 all-gather.4.cloned.1.call-start
  7.2 0.7 all-gather.4.cloned.1.call-update
  7.9 0.0 all-gather.6.cloned.1.call-start
  7.9 1.7 %copy.11 = bf16[3,128,256]{1,2,0:T(8,128)(2,1)} copy(bf16[3,128,256]{2,1,0:T(8,128)(2,1)} %param.8) | data formatting | bytes 393216 | tf_op args[2]
  9.7 0.0 all-gather.6.cloned.1.call-update
  9.7 0.0 reduce-scatter.2.cloned.1.call-start
  9.8 0.7 reshape.34
  10.4 12.6 %all-gather = bf16[4,1,256]{2,1,0:T(2,128)(2,1)S(1)} all-gather(bf16[1,1,256]{2,1,0:T(2,128)(2,1)S(1)} %reshape.34), channel_id=1, replica_groups=mesh['dp'=8,'mp'=4] {'mp'}, dimensions={0}, use_global_device_ids=true | all-gather | bytes 2560 | tf_op jit(solution)/shard_map/all_gather | solution.py:45
  23.1 0.0 copy-start.2
  23.1 2.8 %copy.12 = bf16[4,512,512]{1,2,0:T(8,128)(2,1)S(1)} copy(bf16[4,512,512]{2,1,0:T(8,128)(2,1)} %param.10) | data formatting | bytes 4194304 | tf_op args[4]
  25.9 0.0 copy-done.2
  25.9 10.0 %all_gather.15 = bf16[256,1024]{1,0:T(8,128)(2,1)S(1)} all-gather(bf16[256,128]{1,0:T(8,128)(2,1)S(1)} %copy-done.2), channel_id=1, replica_groups=mesh['dp'=8,'mp'=4] {'dp'}, dimensions={1}, use_global_device_ids=true | all-gather | bytes 589824 | tf_op jit(solution)/shard_map/all_gather | solution.py:60
  35.9 6.2 %all-gather.4.cloned.1.call-done = bf16[512,1024]{1,0:T(8,128)(2,1)} async-done(((bf16[512,256]{1,0:T(8,128)(2,1)}), bf16[512,1024]{1,0:T(8,128)(2,1)}) %all-gather.4.cloned.1.call-update) | async-done | bytes 1048592 | tf_op jit(solution)/shard_map/all_gather | solution.py:44
  42.1 1.5 %fusion.2 = f32[512]{0:T(512)S(1)} fusion(bf16[512,1024]{1,0:T(8,128)(2,1)} %all-gather.4.cloned.1.call-done), kind=kLoop, calls=%fused_computation.7 | loop fusion | flops 1572352 | bytes 1050624 | tf_op jit(solution)/shard_map/reduce_sum | solution.py:48
  43.6 25.1 %all-gather.6.cloned.1.call-done = bf16[3,1024,256]{1,2,0:T(8,128)(2,1)} async-done(((bf16[3,128,256]{1,2,0:T(8,128)(2,1)}), bf16[3,1024,256]{1,2,0:T(8,128)(2,1)}) %all-gather.6.cloned.1.call-update) | async-done | bytes 1572880 | tf_op jit(solution)/shard_map/all_gather | solution.py:54
  68.7 2.8 %fusion.6 = bf16[3,512,256]{1,2,0:T(8,128)(2,1)S(1)} fusion(bf16[3,1024,256]{1,2,0:T(8,128)(2,1)} %all-gather.6.cloned.1.call-done, bf16[512,1024]{1,0:T(8,128)(2,1)} %all-gather.4.cloned.1.call-done, f32[1024]{0:T(1024)S(1)} %bitcast.26, f32[512]{0:T(512)S(1)} %add_rsqrt_fusion.1), kind=kOutput, calls=%fused_computation.13 | convolution fusion | flops 807796736 | bytes 3414016 | tf_op jit(solution)/shard_map/td,kdi->kti/dot_general | solution.py:51
  71.5 0.8 fusion.18
  72.3 1.5 %fusion.19 = f32[4,512]{1,0:T(4,128)S(1)} fusion(bf16[4,512,512]{1,2,0:T(8,128)(2,1)S(1)} %copy.12, bf16[512,4,64]{0,2,1:T(8,128)(2,1)S(1)} %bitcast.23, bf16[512,4,64]{0,2,1:T(8,128)(2,1)S(1)} %bitcast.21), kind=kOutput, calls=%fused_computation.29 | convolution fusion | flops 138412544 | bytes 2629632 | tf_op jit(solution)/shard_map/while/body/eval_jaxpr/sub | solution.py:31
  73.8 2.9 %fusion.7 = bf16[4,64,512]{2,1,0:T(8,128)(2,1)S(1)} fusion(bf16[512,4,64]{0,2,1:T(8,128)(2,1)} %bitcast.25, f32[4,512]{1,0:T(4,128)S(1)} %fusion.19, bf16[4,512,512]{1,2,0:T(8,128)(2,1)S(1)} %copy.12, bf16[512,4,64]{0,2,1:T(8,128)(2,1)S(1)} %bitcast.24, bf16[512,4,64]{0,2,1:T(8,128)(2,1)S(1)} %bitcast.22), kind=kOutput, calls=%fused_computation.14 | convolution fusion | flops 273811968 | bytes 3153920 | tf_op jit(solution)/shard_map/while/body/eval_jaxpr/hqk,khd->qhd/dot_general | solution.py:33
  76.6 0.0 copy-start.3
  76.6 0.0 copy-start.1
  76.6 1.4 %convolution_convert_fusion = bf16[512,1024]{1,0:T(8,128)(2,1)} fusion(bf16[512,256]{0,1:T(8,128)(2,1)S(1)} %bitcast.20, bf16[256,1024]{1,0:T(8,128)(2,1)S(1)} %all_gather.15), kind=kOutput, calls=%fused_computation.11 | convolution fusion | flops 268959744 | bytes 1835008 | tf_op jit(solution)/shard_map/dot_general | solution.py:58
  78.1 0.0 reduce-scatter.2.cloned.1.call-update
  78.1 0.0 copy-done.3
  78.1 27.4 %reduce-scatter.2.cloned.1.call-done = bf16[512,256]{1,0:T(8,128)(2,1)} async-done(((bf16[512,1024]{1,0:T(8,128)(2,1)}), bf16[512,256]{1,0:T(8,128)(2,1)}) %reduce-scatter.2.cloned.1.call-update) | async-done | bytes 262160 | tf_op jit(solution)/shard_map/reduce_scatter | solution.py:63
  105.6 0.0 copy-done.1
  105.6 1.0 add_convert_fusion
  106.6 0.0 copy-start
  106.6 0.1 fusion.12
  106.7 9.3 %psum.7 = f32[512]{0:T(512)S(1)} all-reduce(f32[512]{0:T(512)S(1)} %fusion.12), channel_id=1, replica_groups=mesh['dp'=8,'mp'=4] {'mp'}, use_global_device_ids=true, to_apply=%region_5.6 | all-reduce | flops 512 | bytes 4096 | tf_op jit(solution)/shard_map/psum | solution.py:68
  116.0 0.8 fusion.14
  116.9 0.0 copy-done
  (4 shorter events, 0.0 us)
Async XLA Ops:
  7.2 35.0 %all-gather.4.cloned.1.call-start = ((), (), s32[]{:S(2)}) async-start(), calls=%async_computation.1 | async-start | bytes 1310720 | tf_op jit(solution)/shard_map/all_gather | solution.py:44
  7.9 60.8 %all-gather.6.cloned.1.call-start = ((), (), s32[]{:S(2)}) async-start(), calls=%async_computation.2 | async-start | bytes 1769472 | tf_op jit(solution)/shard_map/all_gather | solution.py:54
  9.7 95.8 %reduce-scatter.2.cloned.1.call-start = ((), (), s32[]{:S(2)}) async-start(), calls=%async_computation.3 | async-start | bytes 1310720 | tf_op jit(solution)/shard_map/reduce_scatter | solution.py:63
  23.1 2.8 %copy-start.2 = (bf16[256,128]{1,0:T(8,128)(2,1)S(1)}, bf16[256,128]{1,0:T(8,128)(2,1)}, u32[]{:S(2)}) copy-start(bf16[256,128]{1,0:T(8,128)(2,1)} %param.9) | copy-start | bytes 196612
  76.6 1.5 %copy-start.3 = (bf16[256]{0:T(256)(128)(2,1)S(1)}, bf16[256]{0:T(256)(128)(2,1)}, u32[]{:S(2)}) copy-start(bf16[256]{0:T(256)(128)(2,1)} %param.11) | copy-start | bytes 1540
  76.6 28.9 %copy-start.1 = (bf16[512,256]{1,0:T(8,128)(2,1)S(1)}, bf16[512,256]{1,0:T(8,128)(2,1)}, u32[]{:S(2)}) copy-start(bf16[512,256]{1,0:T(8,128)(2,1)} %param.6) | copy-start | bytes 786436
  106.6 10.3 %copy-start = (bf16[512,256]{1,0:T(8,128)(2,1)}, bf16[512,256]{1,0:T(8,128)(2,1)S(1)}, u32[]{:S(2)}) copy-start(bf16[512,256]{1,0:T(8,128)(2,1)S(1)} %add_convert_fusion) | copy-start | bytes 786436
Sparse Core Ops, SparseCore 0:
  9.5 32.5 all-gather.3
  44.6 24.0 all-gather.5
  78.2 27.2 reduce-scatter.1
where the time goes:
time: 124 us; the launch traced here: 123 us
  waiting for transfers between devices  59.4 us (48%)
  blocking collectives  31.9 us (26%)
  between operations  13.8 us (11%)
  matrix products  8.6 us (7%)
  local copies, waits for them, and re-layouts  6 us (5%)
  other arithmetic  3.54 us (3%)
    reduce_scatter x1, waiting for transfers between devices, on_device(): lax.psum_scatter(partial_value.astype(jnp.bfloat16), 'mp', scatter_dimens...  27.4 us
    all_gather x1, waiting for transfers between devices, on_device(): lax.all_gather(input_weight, 'dp', axis=1, tiled=True)  25.1 us
    all_gather x1, blocking collectives, on_device(): lax.all_gather(pre_gain, 'mp', axis=0, tiled=True)  12.6 us
    all_gather x1, blocking collectives, on_device(): lax.all_gather(output_weight, 'dp', axis=1, tiled=True)  9.99 us
    psum x1, blocking collectives, on_device(): squares = lax.psum(jnp.sum(restored * restored, axis=1), 'mp')  9.28 us
    all_gather x1, waiting for transfers between devices, on_device(): lax.all_gather(tokens, 'mp', axis=1, tiled=True)  6.23 us
    unnamed x11, local copies, waits for them, and re-layouts  5.24 us
    dot_general x1, matrix products, one_sequence(): jnp.einsum('hqk,khd->qhd', probabilities, sequence_block[2], preferred_el...  2.86 us
  transfers between devices with their start and end apart: 3, of which 3 were waited for; matrix products, arithmetic and copies ran while one was open for 5% of the time, Pallas kernels for 0%

commit v1 on v0

v1 whole, which is shorter than its diff:
```python
import functools

import jax
import jax.numpy as jnp
from jax import lax
from jax.experimental import pallas as pl
from jax.experimental.pallas import tpu as pltpu
from jax.sharding import PartitionSpec as P

epsilon = 1e-06
F32, BF16 = jnp.float32, jnp.bfloat16


def kernel(
    n,
    groups,
    chunks,
    wide,
    tok,
    gains,
    win,
    wout,
    bias,
    stream_o,
    normed_o,
    x_all,
    gain_all,
    w_all,
    wo_all,
    bias_v,
    acc,
    square,
    qkv,
    part,
    out_buf,
    from_below,
    from_above,
    ss_mine,
    ss_all,
    ag_send,
    ag_recv,
    g_send,
    g_recv,
    w_send,
    w_recv,
    o_send,
    o_recv,
    rs_send,
    rs_recv,
    ss_send,
    ss_recv,
    local_sem,
):
    rows, feats = tok.shape
    step = rows // chunks
    heads, seq = bias.shape[0], bias.shape[1]
    inner = win.shape[2]
    head_dim = inner // heads
    model = n * feats
    wrows = win.shape[1]
    wcols = model // groups
    half = groups // 2
    me = lax.axis_index("mp")
    d = lax.axis_index("dp")
    odd = lax.rem(d, 2)
    pair = d // 2
    partner = d + 1 - 2 * odd

    def rows_at(c):
        return pl.ds(pl.multiple_of(c * step, step), step)

    def tok_copy(s, c, up, own):
        src = tok.at[rows_at(c)] if own else x_all.at[s, rows_at(c)]
        return pltpu.make_async_remote_copy(
            src_ref=src,
            dst_ref=x_all.at[s, rows_at(c)],
            send_sem=ag_send.at[up, s, c],
            recv_sem=ag_recv.at[s, c],
            device_id={"mp": me + 2 * up - 1},
            device_id_type=pl.DeviceIdType.MESH,
        )

    def gain_copy(origin, target):
        return pltpu.make_async_remote_copy(
            src_ref=gains,
            dst_ref=gain_all.at[origin],
            send_sem=g_send.at[target],
            recv_sem=g_recv.at[origin],
            device_id={"mp": target},
            device_id_type=pl.DeviceIdType.MESH,
        )

    def w_slot(o):
        return w_all.at[:, pl.ds(pl.multiple_of(o * wrows, wrows), wrows), :]

    def o_slot(o):
        block = pl.ds(pl.multiple_of(o * wcols, wcols), wcols)
        return wo_all.at[:, block] if wide else wo_all.at[block, :]

    def weight_copy(which, o, target, forward):
        slot, ref, send, recv = (
            (w_slot, win, w_send, w_recv) if which == 0 else (o_slot, wout, o_send, o_recv)
        )
        return pltpu.make_async_remote_copy(
            src_ref=slot(o) if forward else ref,
            dst_ref=slot(o),
            send_sem=send.at[1, o] if forward else send.at[0, target],
            recv_sem=recv.at[o],
            device_id={"dp": target},
            device_id_type=pl.DeviceIdType.MESH,
        )

    def rs_copy(s, c, up):
        return pltpu.make_async_remote_copy(
            src_ref=out_buf.at[s, rows_at(c)],
            dst_ref=(from_below if up else from_above).at[s, rows_at(c)],
            send_sem=rs_send.at[s, c],
            recv_sem=rs_recv.at[up, s, c],
            device_id={"mp": me + 2 * up - 1},
            device_id_type=pl.DeviceIdType.MESH,
        )

    def ss_copy(origin, c, target):
        return pltpu.make_async_remote_copy(
            src_ref=ss_mine.at[c],
            dst_ref=ss_all.at[origin, c],
            send_sem=ss_send.at[target, c],
            recv_sem=ss_recv.at[origin, c],
            device_id={"mp": target},
            device_id_type=pl.DeviceIdType.MESH,
        )

    def loop(count, body, start=0):
        def wrapped(i, carry):
            body(i)
            return carry

        lax.fori_loop(start, count, wrapped, 0)

    def local_copies():
        return (
            pltpu.make_async_copy(win, w_slot(d), local_sem.at[0]),
            pltpu.make_async_copy(wout, o_slot(d), local_sem.at[1]),
            pltpu.make_async_copy(tok, x_all.at[me], local_sem.at[2]),
            pltpu.make_async_copy(gains, gain_all.at[me], local_sem.at[3]),
            pltpu.make_async_copy(bias, bias_v, local_sem.at[4]),
        )

    for copy in local_copies():
        copy.start()

    barrier = pltpu.get_barrier_semaphore()

    def greet_mp(k):
        pl.semaphore_signal(
            barrier,
            inc=1,
            device_id={"mp": lax.rem(me + k, n)},
            device_id_type=pl.DeviceIdType.MESH,
        )

    def greet_dp(k):
        pl.semaphore_signal(
            barrier,
            inc=1,
            device_id={"dp": lax.rem(d + k, groups)},
            device_id_type=pl.DeviceIdType.MESH,
        )

    loop(n, greet_mp, 1)
    loop(groups, greet_dp, 1)
    pl.semaphore_wait(barrier, n - 1 + groups - 1)

    def peer_mp(k):
        return lax.rem(me + k, n)

    def same_core(k):
        return 2 * lax.rem(pair + k, half) + odd

    def from_core(k):
        return 2 * lax.rem(pair + half - k, half) + odd

    loop(n, lambda k: gain_copy(me, peer_mp(k)).start(), 1)
    for c in range(chunks):

        @pl.when(me < n - 1)
        def _():
            tok_copy(me, c, 1, True).start()

        @pl.when(me > 0)
        def _():
            tok_copy(me, c, 0, True).start()

    weight_copy(0, d, partner, False).start()
    loop(half, lambda k: weight_copy(0, d, same_core(k), False).start(), 1)
    weight_copy(1, d, partner, False).start()
    loop(half, lambda k: weight_copy(1, d, same_core(k), False).start(), 1)

    acc[...] = jnp.zeros_like(acc)
    square[...] = jnp.zeros_like(square)

    def take_shards(j):
        below, above = me - j, me + j

        def one(c):
            @pl.when(below >= 0)
            def _():
                tok_copy(below, c, 1, False).wait_recv()

                @pl.when(me < n - 1)
                def _():
                    tok_copy(below, c, 1, False).start()

            @pl.when(above < n)
            def _():
                tok_copy(above, c, 0, False).wait_recv()

                @pl.when(me > 0)
                def _():
                    tok_copy(above, c, 0, False).start()

        loop(chunks, one)

    def project(j):
        def side(up):
            s = me + (2 * up - 1) * j

            @pl.when((s >= 0) & (s < n) & ((j > 0) | (up == 0)))
            def _():
                block = pl.ds(pl.multiple_of(s * feats, feats), feats)
                gain = gain_all[s][0:1, :]

                def piece(c):
                    x = x_all[s, rows_at(c), :].astype(F32)
                    square[rows_at(c), :] += x * x
                    xg = (x * gain).astype(BF16)
                    for m in range(3):
                        acc[m, rows_at(c), :] += jnp.dot(
                            xg, w_all[m, block, :], preferred_element_type=F32
                        )

                loop(chunks, piece)

        loop(2, side)

    def weights_in(which):
        def forward(k):
            o = from_core(k)
            weight_copy(which, o, partner, False).wait_recv()
            weight_copy(which, o, partner, True).start()

        loop(half, forward, 1)

        def others(k):
            weight_copy(which, 2 * k + 1 - odd, partner, False).wait_recv()

        loop(half, others)

    take_shards(1)
    for copy in local_copies():
        copy.wait()
    loop(n, lambda k: gain_copy(peer_mp(k), peer_mp(k)).wait_recv(), 1)
    weights_in(0)
    loop(2, project)

    def later(j):
        take_shards(j)
        project(j)

    loop(n, later, 2)
    weights_in(1)

    def finish(c):
        total = jnp.sum(square[rows_at(c), :], axis=1, keepdims=True)
        inverse = lax.rsqrt(total / model + epsilon)
        for m in range(3):
            qkv[m, rows_at(c), :] = (acc[m, rows_at(c), :] * inverse).astype(BF16)

    loop(chunks, finish)

    lane_head = lax.broadcasted_iota(jnp.int32, (1, inner), 1) // head_dim
    contract = (((1,), (1,)), ((), ()))

    def send_out(s, c, up, value):
        out_buf[s, rows_at(c), :] = value.astype(BF16)
        rs_copy(s, c, up).start()

    def attend(c):
        first = (c * step) // seq * seq
        keys_at = pl.ds(pl.multiple_of(first, seq), seq)
        bias_at = pl.ds(pl.multiple_of(c * step - first, step), step)
        q = qkv[0, rows_at(c), :]
        k = qkv[1, keys_at, :]
        v = qkv[2, keys_at, :]
        context = jnp.zeros((step, inner), F32)
        for h in range(heads):
            qh = jnp.where(lane_head == h, q, jnp.zeros_like(q))
            scores = lax.dot_general(qh, k, contract, preferred_element_type=F32)
            scores = scores + bias_v[h, bias_at, :].astype(F32)
            weights = jnp.exp(scores - jnp.max(scores, axis=1, keepdims=True))
            scale = 1.0 / jnp.sum(weights, axis=1, keepdims=True)
            mixed = jnp.dot(weights.astype(BF16), v, preferred_element_type=F32)
            context = jnp.where(lane_head == h, mixed * scale, context)
        context = context.astype(BF16)

        def share(s):
            block = pl.ds(pl.multiple_of(s * feats, feats), feats)
            if wide:
                value = jnp.dot(context, wo_all[:, block], preferred_element_type=F32)
            else:
                value = lax.dot_general(
                    context, wo_all[block, :], contract, preferred_element_type=F32
                )
            part[s, rows_at(c), :] = value

        for s in range(n):
            share(s)

        @pl.when(me == 0)
        def _():
            loop(n - 1, lambda k: send_out(n - 1 - k, c, 1, part[n - 1 - k, rows_at(c), :]))

        @pl.when(me == n - 1)
        def _():
            loop(n - 1, lambda k: send_out(k, c, 0, part[k, rows_at(c), :]))

    loop(rows // step, attend)

    def reduce(c):
        def hop(k):
            up_s, down_s = n - 1 - k, k

            @pl.when((up_s > me) & (me > 0))
            def _():
                rs_copy(up_s, c, 1).wait_recv()
                send_out(
                    up_s,
                    c,
                    1,
                    part[up_s, rows_at(c), :] + from_below[up_s, rows_at(c), :].astype(F32),
                )

            @pl.when((down_s < me) & (me < n - 1))
            def _():
                rs_copy(down_s, c, 0).wait_recv()
                send_out(
                    down_s,
                    c,
                    0,
                    part[down_s, rows_at(c), :] + from_above[down_s, rows_at(c), :].astype(F32),
                )

        loop(n - 1, hop)

        @pl.when(me > 0)
        def _():
            rs_copy(me, c, 1).wait_recv()
            part[me, rows_at(c), :] += from_below[me, rows_at(c), :].astype(F32)

        @pl.when(me < n - 1)
        def _():
            rs_copy(me, c, 0).wait_recv()
            part[me, rows_at(c), :] += from_above[me, rows_at(c), :].astype(F32)

        stream = (x_all[me, rows_at(c), :].astype(F32) + part[me, rows_at(c), :]).astype(BF16)
        stream_o[rows_at(c), :] = stream
        wide_stream = stream.astype(F32)
        total = jnp.sum(wide_stream * wide_stream, axis=1, keepdims=True)
        turned = jnp.transpose(jnp.broadcast_to(total, (step, 128)))
        ss_mine[c] = turned[0:8, :]
        ss_all[me, c] = turned[0:8, :]
        loop(n, lambda k: ss_copy(me, c, peer_mp(k)).start(), 1)

    loop(chunks, reduce)

    def normalize(c):
        loop(n, lambda k: ss_copy(peer_mp(k), c, peer_mp(k)).wait_recv(), 1)
        total = jnp.zeros((8, step), F32)
        for s in range(n):
            total = total + ss_all[s, c]
        post = jnp.transpose(lax.rsqrt(total / model + epsilon))[:, 0:1]
        stream = stream_o[rows_at(c), :].astype(F32)
        gain = gain_all[me][1:2, :]
        normed_o[rows_at(c), :] = (stream * post * gain).astype(BF16)

    loop(chunks, normalize)

    loop(n, lambda k: gain_copy(me, peer_mp(k)).wait_send(), 1)

    def drain_tokens(s):
        def one(c):
            @pl.when((s <= me) & (me < n - 1))
            def _():
                tok_copy(s, c, 1, False).wait_send()

            @pl.when((s >= me) & (me > 0))
            def _():
                tok_copy(s, c, 0, False).wait_send()

            @pl.when(s != me)
            def _():
                rs_copy(s, c, 1).wait_send()
                ss_copy(me, c, s).wait_send()

        loop(chunks, one)

    loop(n, drain_tokens)
    for which in range(2):
        weight_copy(which, d, partner, False).wait_send()

        def drain(k):
            weight_copy(which, d, same_core(k), False).wait_send()
            weight_copy(which, from_core(k), partner, True).wait_send()

        loop(half, drain, 1)


def on_device(n, groups, tokens, pre_gain, input_weight, output_weight, position_bias, post_gain):
    rows, feats = tokens.shape
    chunks = rows // 128
    step = rows // chunks
    inner = input_weight.shape[2]
    model = n * feats
    wide = output_weight.shape[1] % 128 == 0
    gains = jnp.stack([pre_gain, post_gain]).astype(F32)
    if not wide:
        output_weight = output_weight.T
    dma, any_space = pltpu.SemaphoreType.DMA, pl.BlockSpec(memory_space=pl.ANY)
    shape = jax.ShapeDtypeStruct((rows, feats), BF16)
    return pl.pallas_call(
        functools.partial(kernel, n, groups, chunks, wide),
        out_shape=(shape, shape),
        in_specs=[any_space] * 5,
        out_specs=[pl.BlockSpec(memory_space=pltpu.VMEM)] * 2,
        scratch_shapes=[
            pltpu.VMEM((n, rows, feats), BF16),
            pltpu.VMEM((n, 2, feats), F32),
            pltpu.VMEM((3, model, inner), BF16),
            pltpu.VMEM((inner, model) if wide else (model, inner), BF16),
            pltpu.VMEM(position_bias.shape, BF16),
            pltpu.VMEM((3, rows, inner), F32),
            pltpu.VMEM((rows, feats), F32),
            pltpu.VMEM((3, rows, inner), BF16),
            pltpu.VMEM((n, rows, feats), F32),
            pltpu.VMEM((n, rows, feats), BF16),
            pltpu.VMEM((n, rows, feats), BF16),
            pltpu.VMEM((n, rows, feats), BF16),
            pltpu.VMEM((chunks, 8, step), F32),
            pltpu.VMEM((n, chunks, 8, step), F32),
            dma((2, n, chunks)),
            dma((n, chunks)),
            dma((n,)),
            dma((n,)),
            dma((2, groups)),
            dma((groups,)),
            dma((2, groups)),
            dma((groups,)),
            dma((n, chunks)),
            dma((2, n, chunks)),
            dma((n, chunks)),
            dma((n, chunks)),
            dma((5,)),
        ],
        compiler_params=pltpu.CompilerParams(
            collective_id=0, has_side_effects=True, vmem_limit_bytes=56 * 1024 * 1024
        ),
    )(tokens, gains, input_weight, output_weight, position_bias)


def solution(mesh):
    return jax.shard_map(
        functools.partial(on_device, mesh.shape["mp"], mesh.shape["dp"]),
        mesh=mesh,
        in_specs=(
            P("dp", "mp"),
            P("mp"),
            P(None, "dp", "mp"),
            P("mp", "dp"),
            P("mp", None, None),
            P("mp"),
        ),
        out_specs=(P("dp", "mp"), P("dp", "mp")),
        check_vma=False,
    )
```

time: 124 us -> 82.1 us (0.66)
  Pallas kernels: 0 us -> 76 us
  waiting for transfers between devices: 59.4 us -> 0 us
  blocking collectives: 31.9 us -> 0 us
  between operations: 13.8 us -> 0.64 us
  matrix products: 8.6 us -> 0 us
  other arithmetic: 3.54 us -> 0.59 us
  local copies, waits for them, and re-layouts: 6 us -> 4.66 us
    pallas_call x0 -> x1, Pallas kernels: none -> 76 us  [on_device(): pl.pallas_call(functools.partial(kernel, n, groups, chunks, wide), out_sh...]
    all_gather x2 -> x0, waiting for transfers between devices: 31.3 us -> none  [the longest x1 25.1 us: on_device(): lax.all_gather(input_weight, 'dp', axis=1, tiled=True)]
    reduce_scatter x1 -> x0, waiting for transfers between devices: 27.4 us -> none  [on_device(): lax.psum_scatter(partial_value.astype(jnp.bfloat16), 'mp', scatter_dimens...]
    all_gather x2 -> x0, blocking collectives: 22.6 us -> none  [the longest x1 12.6 us: on_device(): lax.all_gather(pre_gain, 'mp', axis=0, tiled=True)]
    psum x1 -> x0, blocking collectives: 9.28 us -> none  [on_device(): squares = lax.psum(jnp.sum(restored * restored, axis=1), 'mp')]
    dot_general x3 -> x0, matrix products: 7.13 us -> none  [the longest x1 2.86 us: one_sequence(): jnp.einsum('hqk,khd->qhd', probabilities, sequence_block[2], preferred_el...]
    unnamed x11 -> x2, local copies, waits for them, and re-layouts: 5.24 us -> 3.34 us
    reduce_sum x2 -> x0, other arithmetic: 1.65 us -> none  [the longest x1 1.5 us: on_device(): jnp.mean(widened * widened, axis=1, keepdims=True) + epsilon]
  transfers between devices with their start and end apart: 3 -> 0, of which waited for: 3 -> 0; matrix products, arithmetic and copies ran while one was open for 5% -> 0% of each run, Pallas kernels for 0% -> 0%
where the time goes in v1:
time: 82.1 us; the launch traced here: 81.9 us
  Pallas kernels  76 us (93%)
  local copies, waits for them, and re-layouts  4.66 us (6%)
    pallas_call x1, Pallas kernels, on_device(): pl.pallas_call(functools.partial(kernel, n, groups, chunks, wide), out_sh...  76 us
    unnamed x2, local copies, waits for them, and re-layouts  3.34 us

profile of v1, /device:TPU:0, one launch (start us, length us, event | category | flops | bytes accessed | tf_op | source)
XLA Modules:
  0.0 81.9 jit_solution(4949762495694268206)
XLA Ops:
  0.6 0.7 stack.9
  1.3 0.7 stack.10
  1.9 0.6 maximum_convert_fusion.gains
  2.5 76.0 %shard_map.77 = (bf16[512,256]{1,0:T(8,128)(2,1)}, bf16[512,256]{1,0:T(8,128)(2,1)}) custom-call(bf16[512,256]{1,0:T(8,128)(2,1)} %tok.1, f32[2,256]{1,0:T(2,128)} %maximum_convert_fusion.gains, bf16[3,128,256]{2,1,0:T(8,128)(2,1)} %win.1, bf16[256,128]{1,0:T(8,128)(2,1)} %wout.1, bf16[4,512,512]{2,1,0:T(8,128)(2,1)} %bias.1), custom_call_target="tpu_custom_call" | custom-call | tf_op jit(solution)/shard_map/pallas_call | solution.py:430
  78.5 1.7 %copy.10 = bf16[512,256]{1,0:T(8,128)(2,1)} copy(bf16[512,256]{1,0:T(8,128)(2,1)} %get-tuple-element.4) | data formatting | bytes 524288
  80.2 1.7 %copy.11 = bf16[512,256]{1,0:T(8,128)(2,1)} copy(bf16[512,256]{1,0:T(8,128)(2,1)} %get-tuple-element.5) | data formatting | bytes 524288

commit v2 on v1

--- a/solution.py
+++ b/solution.py
@@ -15,9 +15,11 @@
     n,
     groups,
     chunks,
+    lag,
     wide,
     tok,
-    gains,
+    pre,
+    post_g,
     win,
     wout,
     bias,
@@ -69,6 +71,9 @@
     def rows_at(c):
         return pl.ds(pl.multiple_of(c * step, step), step)
 
+    def feats_at(s):
+        return pl.ds(pl.multiple_of(s * feats, feats), feats)
+
     def tok_copy(s, c, up, own):
         src = tok.at[rows_at(c)] if own else x_all.at[s, rows_at(c)]
         return pltpu.make_async_remote_copy(
@@ -82,8 +87,8 @@
 
     def gain_copy(origin, target):
         return pltpu.make_async_remote_copy(
-            src_ref=gains,
-            dst_ref=gain_all.at[origin],
+            src_ref=pre,
+            dst_ref=gain_all.at[feats_at(origin)],
             send_sem=g_send.at[target],
             recv_sem=g_recv.at[origin],
             device_id={"mp": target},
@@ -142,7 +147,7 @@
             pltpu.make_async_copy(win, w_slot(d), local_sem.at[0]),
             pltpu.make_async_copy(wout, o_slot(d), local_sem.at[1]),
             pltpu.make_async_copy(tok, x_all.at[me], local_sem.at[2]),
-            pltpu.make_async_copy(gains, gain_all.at[me], local_sem.at[3]),
+            pltpu.make_async_copy(pre, gain_all.at[feats_at(me)], local_sem.at[3]),
             pltpu.make_async_copy(bias, bias_v, local_sem.at[4]),
         )
 
@@ -227,19 +232,14 @@
 
             @pl.when((s >= 0) & (s < n) & ((j > 0) | (up == 0)))
             def _():
-                block = pl.ds(pl.multiple_of(s * feats, feats), feats)
-                gain = gain_all[s][0:1, :]
-
-                def piece(c):
-                    x = x_all[s, rows_at(c), :].astype(F32)
-                    square[rows_at(c), :] += x * x
-                    xg = (x * gain).astype(BF16)
-                    for m in range(3):
-                        acc[m, rows_at(c), :] += jnp.dot(
-                            xg, w_all[m, block, :], preferred_element_type=F32
-                        )
-
-                loop(chunks, piece)
+                block = feats_at(s)
+                gain = gain_all[feats_at(s)].astype(F32).reshape(1, feats)
+
+                x = x_all[s].astype(F32)
+                square[...] += x * x
+                xg = (x * gain).astype(BF16)
+                for m in range(3):
+                    acc[m] += jnp.dot(xg, w_all[m, block, :], preferred_element_type=F32)
 
         loop(2, side)
 
@@ -304,7 +304,7 @@
         context = context.astype(BF16)
 
         def share(s):
-            block = pl.ds(pl.multiple_of(s * feats, feats), feats)
+            block = feats_at(s)
             if wide:
                 value = jnp.dot(context, wo_all[:, block], preferred_element_type=F32)
             else:
@@ -326,43 +326,9 @@
 
     loop(rows // step, attend)
 
-    def reduce(c):
-        def hop(k):
-            up_s, down_s = n - 1 - k, k
-
-            @pl.when((up_s > me) & (me > 0))
-            def _():
-                rs_copy(up_s, c, 1).wait_recv()
-                send_out(
-                    up_s,
-                    c,
-                    1,
-                    part[up_s, rows_at(c), :] + from_below[up_s, rows_at(c), :].astype(F32),
-                )
-
-            @pl.when((down_s < me) & (me < n - 1))
-            def _():
-                rs_copy(down_s, c, 0).wait_recv()
-                send_out(
-                    down_s,
-                    c,
-                    0,
-                    part[down_s, rows_at(c), :] + from_above[down_s, rows_at(c), :].astype(F32),
-                )
-
-        loop(n - 1, hop)
-
-        @pl.when(me > 0)
-        def _():
-            rs_copy(me, c, 1).wait_recv()
-            part[me, rows_at(c), :] += from_below[me, rows_at(c), :].astype(F32)
-
-        @pl.when(me < n - 1)
-        def _():
-            rs_copy(me, c, 0).wait_recv()
-            part[me, rows_at(c), :] += from_above[me, rows_at(c), :].astype(F32)
-
-        stream = (x_all[me, rows_at(c), :].astype(F32) + part[me, rows_at(c), :]).astype(BF16)
+    def finalize(c):
+        own = x_all[me, rows_at(c), :].astype(F32) + part[me, rows_at(c), :]
+        stream = own.astype(BF16)
         stream_o[rows_at(c), :] = stream
         wide_stream = stream.astype(F32)
         total = jnp.sum(wide_stream * wide_stream, axis=1, keepdims=True)
@@ -371,7 +337,55 @@
         ss_all[me, c] = turned[0:8, :]
         loop(n, lambda k: ss_copy(me, c, peer_mp(k)).start(), 1)
 
-    loop(chunks, reduce)
+    messages = chunks * (n - 1)
+
+    def chain(t, up, lead):
+        m = t - lead
+        landed = from_below if up else from_above
+
+        @pl.when((m >= 0) & (m < messages))
+        def _():
+            c, k = m // (n - 1), lax.rem(m, n - 1)
+            s = n - 1 - k if up else k
+            further = s > me if up else s < me
+
+            @pl.when(further | (s == me))
+            def _():
+                rs_copy(s, c, up).wait_recv()
+                value = part[s, rows_at(c), :] + landed[s, rows_at(c), :].astype(F32)
+
+                @pl.when(s == me)
+                def _():
+                    part[s, rows_at(c), :] = value
+
+                @pl.when(further)
+                def _():
+                    send_out(s, c, up, value)
+
+    up_lead, down_lead = (me - 1) * lag, (n - 2 - me) * lag
+    up_last, down_last = n - 1 - me + up_lead, me + down_lead
+    last = jnp.where(
+        me == 0, down_last, jnp.where(me == n - 1, up_last, jnp.maximum(up_last, down_last))
+    )
+
+    def tick(t):
+        @pl.when(me > 0)
+        def _():
+            chain(t, 1, up_lead)
+
+        @pl.when(me < n - 1)
+        def _():
+            chain(t, 0, down_lead)
+
+        @pl.when((t >= last) & (lax.rem(t - last + n - 1, n - 1) == 0))
+        def _():
+            c = (t - last + n - 1) // (n - 1) - 1
+
+            @pl.when(c < chunks)
+            def _():
+                finalize(c)
+
+    loop(messages + (n - 2) * lag, tick)
 
     def normalize(c):
         loop(n, lambda k: ss_copy(peer_mp(k), c, peer_mp(k)).wait_recv(), 1)
@@ -380,7 +394,7 @@
             total = total + ss_all[s, c]
         post = jnp.transpose(lax.rsqrt(total / model + epsilon))[:, 0:1]
         stream = stream_o[rows_at(c), :].astype(F32)
-        gain = gain_all[me][1:2, :]
+        gain = post_g[...].astype(F32).reshape(1, feats)
         normed_o[rows_at(c), :] = (stream * post * gain).astype(BF16)
 
     loop(chunks, normalize)
@@ -417,24 +431,23 @@
 
 def on_device(n, groups, tokens, pre_gain, input_weight, output_weight, position_bias, post_gain):
     rows, feats = tokens.shape
-    chunks = rows // 128
+    chunks, lag = rows // 256, 2
     step = rows // chunks
     inner = input_weight.shape[2]
     model = n * feats
     wide = output_weight.shape[1] % 128 == 0
-    gains = jnp.stack([pre_gain, post_gain]).astype(F32)
     if not wide:
         output_weight = output_weight.T
     dma, any_space = pltpu.SemaphoreType.DMA, pl.BlockSpec(memory_space=pl.ANY)
     shape = jax.ShapeDtypeStruct((rows, feats), BF16)
     return pl.pallas_call(
-        functools.partial(kernel, n, groups, chunks, wide),
+        functools.partial(kernel, n, groups, chunks, lag, wide),
         out_shape=(shape, shape),
-        in_specs=[any_space] * 5,
+        in_specs=[any_space] * 2 + [pl.BlockSpec(memory_space=pltpu.VMEM)] + [any_space] * 3,
         out_specs=[pl.BlockSpec(memory_space=pltpu.VMEM)] * 2,
         scratch_shapes=[
             pltpu.VMEM((n, rows, feats), BF16),
-            pltpu.VMEM((n, 2, feats), F32),
+            pltpu.VMEM((n * feats,), BF16),
             pltpu.VMEM((3, model, inner), BF16),
             pltpu.VMEM((inner, model) if wide else (model, inner), BF16),
             pltpu.VMEM(position_bias.shape, BF16),
@@ -464,7 +477,7 @@
         compiler_params=pltpu.CompilerParams(
             collective_id=0, has_side_effects=True, vmem_limit_bytes=56 * 1024 * 1024
         ),
-    )(tokens, gains, input_weight, output_weight, position_bias)
+    )(tokens, pre_gain, post_gain, input_weight, output_weight, position_bias)
 
 
 def solution(mesh):

time: 82.1 us -> 63.1 us (0.77)
  Pallas kernels: 76 us -> 59 us
  local copies, waits for them, and re-layouts: 4.66 us -> 3.34 us
    pallas_call x1, Pallas kernels: 76 us -> 59 us  [on_device(): pl.pallas_call(functools.partial(kernel, n, groups, chunks, lag, wide), o...]
    another operation x2 -> x0, local copies, waits for them, and re-layouts: 1.32 us -> none  [on_device(): gains = jnp.stack([pre_gain, post_gain]).astype(F32)]
where the time goes in v2:
time: 63.1 us; the launch traced here: 63 us
  Pallas kernels  59 us (94%)
  local copies, waits for them, and re-layouts  3.34 us (5%)
  between operations  0.64 us (1%)
    pallas_call x1, Pallas kernels, on_device(): pl.pallas_call(functools.partial(kernel, n, groups, chunks, lag, wide), o...  59 us
    unnamed x2, local copies, waits for them, and re-layouts  3.34 us

profile of v2, /device:TPU:0, one launch (start us, length us, event | category | flops | bytes accessed | tf_op | source)
XLA Modules:
  0.0 63.0 jit_solution(9128905927246032635)
XLA Ops:
  0.6 59.0 %shard_map.77 = (bf16[512,256]{1,0:T(8,128)(2,1)}, bf16[512,256]{1,0:T(8,128)(2,1)}) custom-call(bf16[512,256]{1,0:T(8,128)(2,1)} %tok.1, bf16[256]{0:T(256)(128)(2,1)} %pre.1, bf16[256]{0:T(256)(128)(2,1)} %post_g.1, bf16[3,128,256]{2,1,0:T(8,128)(2,1)} %win.1, bf16[256,128]{1,0:T(8,128)(2,1)} %wout.1, bf16[4,512,512]{2,1,0:T(8,128)(2,1)} %bias.1), custom_call_target="tpu_custom_call" | custom-call | tf_op jit(solution)/shard_map/pallas_call | solution.py:443
  59.6 1.7 %copy.10 = bf16[512,256]{1,0:T(8,128)(2,1)} copy(bf16[512,256]{1,0:T(8,128)(2,1)} %get-tuple-element.4) | data formatting | bytes 524288
  61.3 1.7 %copy.11 = bf16[512,256]{1,0:T(8,128)(2,1)} copy(bf16[512,256]{1,0:T(8,128)(2,1)} %get-tuple-element.5) | data formatting | bytes 524288

commit v3 on v2

--- a/solution.py
+++ b/solution.py
@@ -52,6 +52,7 @@
     ss_send,
     ss_recv,
     local_sem,
+    link_free,
 ):
     rows, feats = tok.shape
     step = rows // chunks
@@ -186,21 +187,48 @@
         return 2 * lax.rem(pair + half - k, half) + odd
 
     loop(n, lambda k: gain_copy(me, peer_mp(k)).start(), 1)
-    for c in range(chunks):
-
-        @pl.when(me < n - 1)
-        def _():
-            tok_copy(me, c, 1, True).start()
-
-        @pl.when(me > 0)
-        def _():
-            tok_copy(me, c, 0, True).start()
-
+    def send_own(up):
+        @pl.when((me < n - 1) if up else (me > 0))
+        def _():
+            @pl.when(odd == 1)
+            def _():
+                pl.semaphore_wait(link_free.at[up], 1)
+
+            loop(chunks, lambda c: tok_copy(me, c, up, True).start())
+
+    def release(up):
+        s = 0 if up else n - 1
+
+        @pl.when(((me < n - 1) if up else (me > 0)) & (odd == 0))
+        def _():
+            loop(chunks, lambda c: tok_copy(s, c, up, False).wait_send())
+            pl.semaphore_signal(
+                link_free.at[up],
+                inc=1,
+                device_id={"dp": partner},
+                device_id_type=pl.DeviceIdType.MESH,
+            )
+
+    def send_both():
+        @pl.when(2 * me < n)
+        def _():
+            send_own(1)
+            send_own(0)
+
+        @pl.when(2 * me >= n)
+        def _():
+            send_own(0)
+            send_own(1)
+
+    pl.when(odd == 0)(send_both)
     weight_copy(0, d, partner, False).start()
     loop(half, lambda k: weight_copy(0, d, same_core(k), False).start(), 1)
     weight_copy(1, d, partner, False).start()
     loop(half, lambda k: weight_copy(1, d, same_core(k), False).start(), 1)
 
+    pl.when((odd == 0) & (me == 0))(lambda: release(1))
+    pl.when((odd == 0) & (me == n - 1))(lambda: release(0))
+
     acc[...] = jnp.zeros_like(acc)
     square[...] = jnp.zeros_like(square)
 
@@ -225,6 +253,8 @@
                     tok_copy(above, c, 0, False).start()
 
         loop(chunks, one)
+        pl.when((j == me))(lambda: release(1))
+        pl.when((j == n - 1 - me))(lambda: release(0))
 
     def project(j):
         def side(up):
@@ -243,7 +273,7 @@
 
         loop(2, side)
 
-    def weights_in(which):
+    def forward_weights(which):
         def forward(k):
             o = from_core(k)
             weight_copy(which, o, partner, False).wait_recv()
@@ -251,24 +281,34 @@
 
         loop(half, forward, 1)
 
-        def others(k):
-            weight_copy(which, 2 * k + 1 - odd, partner, False).wait_recv()
-
-        loop(half, others)
-
-    take_shards(1)
+    def other_weights(which):
+        loop(half, lambda k: weight_copy(which, 2 * k + 1 - odd, partner, False).wait_recv())
+
+    @pl.when(odd == 1)
+    def _():
+        forward_weights(0)
+        send_both()
+        take_shards(1)
+        forward_weights(1)
+
+    @pl.when(odd == 0)
+    def _():
+        loop(n, take_shards, 1)
+        forward_weights(0)
+
     for copy in local_copies():
         copy.wait()
     loop(n, lambda k: gain_copy(peer_mp(k), peer_mp(k)).wait_recv(), 1)
-    weights_in(0)
+    other_weights(0)
     loop(2, project)
 
     def later(j):
-        take_shards(j)
+        pl.when(odd == 1)(lambda: take_shards(j))
         project(j)
 
     loop(n, later, 2)
-    weights_in(1)
+    pl.when(odd == 0)(lambda: forward_weights(1))
+    other_weights(1)
 
     def finish(c):
         total = jnp.sum(square[rows_at(c), :], axis=1, keepdims=True)
@@ -403,11 +443,11 @@
 
     def drain_tokens(s):
         def one(c):
-            @pl.when((s <= me) & (me < n - 1))
+            @pl.when((s <= me) & (me < n - 1) & ((s > 0) | (odd == 1)))
             def _():
                 tok_copy(s, c, 1, False).wait_send()
 
-            @pl.when((s >= me) & (me > 0))
+            @pl.when((s >= me) & (me > 0) & ((s < n - 1) | (odd == 1)))
             def _():
                 tok_copy(s, c, 0, False).wait_send()
 
@@ -473,6 +513,7 @@
             dma((n, chunks)),
             dma((n, chunks)),
             dma((5,)),
+            pltpu.SemaphoreType.REGULAR((2,)),
         ],
         compiler_params=pltpu.CompilerParams(
             collective_id=0, has_side_effects=True, vmem_limit_bytes=56 * 1024 * 1024

time: 63.1 us -> 58.7 us (0.930)
  the two profiles are of different devices: /device:TPU:0 before, /device:TPU:1 now
where the time goes in v3:
time: 58.7 us; the launch traced here: 58.5 us
  Pallas kernels  54.5 us (93%)
  local copies, waits for them, and re-layouts  3.34 us (6%)
  between operations  0.64 us (1%)
    pallas_call x1, Pallas kernels, on_device(): pl.pallas_call(functools.partial(kernel, n, groups, chunks, lag, wide), o...  54.5 us
    unnamed x2, local copies, waits for them, and re-layouts  3.34 us

profile of v3, /device:TPU:1, one launch (start us, length us, event | category | flops | bytes accessed | tf_op | source)
XLA Modules:
  0.0 58.5 jit_solution(766999201231716709)
XLA Ops:
  0.6 54.5 %shard_map.77 = (bf16[512,256]{1,0:T(8,128)(2,1)}, bf16[512,256]{1,0:T(8,128)(2,1)}) custom-call(bf16[512,256]{1,0:T(8,128)(2,1)} %tok.1, bf16[256]{0:T(256)(128)(2,1)} %pre.1, bf16[256]{0:T(256)(128)(2,1)} %post_g.1, bf16[3,128,256]{2,1,0:T(8,128)(2,1)} %win.1, bf16[256,128]{1,0:T(8,128)(2,1)} %wout.1, bf16[4,512,512]{2,1,0:T(8,128)(2,1)} %bias.1), custom_call_target="tpu_custom_call" | custom-call | tf_op jit(solution)/shard_map/pallas_call | solution.py:483
  55.1 1.7 %copy.10 = bf16[512,256]{1,0:T(8,128)(2,1)} copy(bf16[512,256]{1,0:T(8,128)(2,1)} %get-tuple-element.4) | data formatting | bytes 524288
  56.8 1.7 %copy.11 = bf16[512,256]{1,0:T(8,128)(2,1)} copy(bf16[512,256]{1,0:T(8,128)(2,1)} %get-tuple-element.5) | data formatting | bytes 524288

commit v4 on v3

--- a/solution.py
+++ b/solution.py
@@ -19,12 +19,11 @@
     wide,
     tok,
     pre,
-    post_g,
     win,
     wout,
     bias,
     stream_o,
-    normed_o,
+    square_o,
     x_all,
     gain_all,
     w_all,
@@ -432,10 +431,7 @@
         total = jnp.zeros((8, step), F32)
         for s in range(n):
             total = total + ss_all[s, c]
-        post = jnp.transpose(lax.rsqrt(total / model + epsilon))[:, 0:1]
-        stream = stream_o[rows_at(c), :].astype(F32)
-        gain = post_g[...].astype(F32).reshape(1, feats)
-        normed_o[rows_at(c), :] = (stream * post * gain).astype(BF16)
+        square_o[c] = total
 
     loop(chunks, normalize)
 
@@ -467,6 +463,16 @@
             weight_copy(which, from_core(k), partner, True).wait_send()
 
         loop(half, drain, 1)
+
+
+def post_norm(model, stream_i, square_i, gain_i, stream_o, normed_o):
+    chunks, _, step = square_i.shape
+    gain = gain_i[...].astype(F32).reshape(1, stream_i.shape[1])
+    for c in range(chunks):
+        post = jnp.transpose(lax.rsqrt(square_i[c] / model + epsilon))[:, 0:1]
+        stream = stream_i[c * step : (c + 1) * step, :]
+        stream_o[c * step : (c + 1) * step, :] = stream
+        normed_o[c * step : (c + 1) * step, :] = (stream.astype(F32) * post * gain).astype(BF16)
 
 
 def on_device(n, groups, tokens, pre_gain, input_weight, output_weight, position_bias, post_gain):
@@ -480,10 +486,10 @@
         output_weight = output_weight.T
     dma, any_space = pltpu.SemaphoreType.DMA, pl.BlockSpec(memory_space=pl.ANY)
     shape = jax.ShapeDtypeStruct((rows, feats), BF16)
-    return pl.pallas_call(
+    stream, squares = pl.pallas_call(
         functools.partial(kernel, n, groups, chunks, lag, wide),
-        out_shape=(shape, shape),
-        in_specs=[any_space] * 2 + [pl.BlockSpec(memory_space=pltpu.VMEM)] + [any_space] * 3,
+        out_shape=(shape, jax.ShapeDtypeStruct((chunks, 8, step), F32)),
+        in_specs=[any_space] * 5,
         out_specs=[pl.BlockSpec(memory_space=pltpu.VMEM)] * 2,
         scratch_shapes=[
             pltpu.VMEM((n, rows, feats), BF16),
@@ -518,7 +524,15 @@
         compiler_params=pltpu.CompilerParams(
             collective_id=0, has_side_effects=True, vmem_limit_bytes=56 * 1024 * 1024
         ),
-    )(tokens, pre_gain, post_gain, input_weight, output_weight, position_bias)
+    )(tokens, pre_gain, input_weight, output_weight, position_bias)
+    vmem = pl.BlockSpec(memory_space=pltpu.VMEM)
+    return pl.pallas_call(
+        functools.partial(post_norm, model),
+        out_shape=(shape, shape),
+        in_specs=[vmem] * 3,
+        out_specs=[vmem] * 2,
+        compiler_params=pltpu.CompilerParams(vmem_limit_bytes=8 * 1024 * 1024),
+    )(stream, squares, post_gain)
 
 
 def solution(mesh):

time: 58.7 us -> 57.1 us (0.973)
  local copies, waits for them, and re-layouts: 3.34 us -> 1.66 us
    unnamed x2 -> x6, local copies, waits for them, and re-layouts: 3.34 us -> 1.66 us
    pallas_call x1, Pallas kernels: 54.5 us -> 53.5 us  [on_device(): pl.pallas_call(functools.partial(kernel, n, groups, chunks, lag, wide), o...]
    pallas_call x0 -> x1, Pallas kernels: none -> 0.98 us  [on_device(): pl.pallas_call(functools.partial(post_norm, model), out_shape=(shape, sha...]
where the time goes in v4:
time: 57.1 us; the launch traced here: 56.8 us
  Pallas kernels  54.5 us (95%)
  local copies, waits for them, and re-layouts  1.66 us (3%)
  between operations  0.66 us (1%)
    pallas_call x1, Pallas kernels, on_device(): pl.pallas_call(functools.partial(kernel, n, groups, chunks, lag, wide), o...  53.5 us
    unnamed x6, local copies, waits for them, and re-layouts  1.66 us

profile of v4, /device:TPU:1, one launch (start us, length us, event | category | flops | bytes accessed | tf_op | source)
XLA Modules:
  0.0 56.8 jit_solution(948782587454180523)
XLA Ops:
  0.6 0.0 copy-start.2
  0.6 53.5 %shard_map.77 = (bf16[512,256]{1,0:T(8,128)(2,1)}, f32[2,8,256]{2,1,0:T(8,128)}) custom-call(bf16[512,256]{1,0:T(8,128)(2,1)} %tok.1, bf16[256]{0:T(256)(128)(2,1)} %pre.1, bf16[3,128,256]{2,1,0:T(8,128)(2,1)} %win.1, bf16[256,128]{1,0:T(8,128)(2,1)} %wout.1, bf16[4,512,512]{2,1,0:T(8,128)(2,1)} %bias.1), custom_call_target="tpu_custom_call" | custom-call | tf_op jit(solution)/shard_map/pallas_call | solution.py:489
  54.2 0.0 copy-done.2
  54.2 0.0 copy-start
  54.2 0.9 %copy-done = bf16[512,256]{1,0:T(8,128)(2,1)S(1)} copy-done((bf16[512,256]{1,0:T(8,128)(2,1)S(1)}, bf16[512,256]{1,0:T(8,128)(2,1)}, u32[]{:S(2)}) %copy-start) | copy-done | bytes 262168
  55.1 0.0 copy-start.1
  55.1 0.7 %copy-done.1 = f32[2,8,256]{2,1,0:T(8,128)S(1)} copy-done((f32[2,8,256]{2,1,0:T(8,128)S(1)}, f32[2,8,256]{2,1,0:T(8,128)}, u32[]{:S(2)}) %copy-start.1) | copy-done | bytes 16408
  55.9 1.0 %shard_map.78 = (bf16[512,256]{1,0:T(8,128)(2,1)}, bf16[512,256]{1,0:T(8,128)(2,1)}) custom-call(bf16[512,256]{1,0:T(8,128)(2,1)S(1)} %copy-done, f32[2,8,256]{2,1,0:T(8,128)S(1)} %copy-done.1, bf16[256]{0:T(256)(128)(2,1)S(1)} %copy-done.2), custom_call_target="tpu_custom_call" | custom-call | tf_op jit(solution)/shard_map/pallas_call | solution.py:529
Async XLA Ops:
  0.6 53.5 %copy-start.2 = (bf16[256]{0:T(256)(128)(2,1)S(1)}, bf16[256]{0:T(256)(128)(2,1)}, u32[]{:S(2)}) copy-start(bf16[256]{0:T(256)(128)(2,1)} %gain_i.1) | copy-start | bytes 1540
  54.2 1.0 %copy-start = (bf16[512,256]{1,0:T(8,128)(2,1)S(1)}, bf16[512,256]{1,0:T(8,128)(2,1)}, u32[]{:S(2)}) copy-start(bf16[512,256]{1,0:T(8,128)(2,1)} %get-tuple-element.4.stream_i) | copy-start | bytes 786436
  55.1 0.7 %copy-start.1 = (f32[2,8,256]{2,1,0:T(8,128)S(1)}, f32[2,8,256]{2,1,0:T(8,128)}, u32[]{:S(2)}) copy-start(f32[2,8,256]{2,1,0:T(8,128)} %get-tuple-element.5.square_i) | copy-start | bytes 49156
